TPU v7x, 32 devices: a whole 2x2x4 slice. The times are simulated.
32 devices in a mesh: section: 8 (over z, x), expert: 4 (over y, core).
Axes of the slice: x: 2, y: 2, z: 4, core: 2. Of those that a mesh axis runs over, the one named last changes fastest.
Arguments:
- tokens: bfloat16 [16, 32, 768], P(None, 'expert'), may hold values from -6 to 6
- route_ids: int32 [8, 16, 32, 2], P('section'), may hold values from 0 to 3, all different within a row; in each aligned block of 8 rows (0 to 7, 8 to 15, ..., all dimensions but the last counted through in order) at most 8 rows name the same one
- router: bfloat16 [8, 768, 4], P('section'), may hold values from -0.21875 to 0.21875
- norm_gain: float32 [8, 768], P('section'), may hold values from 0.1 to 1.9
- weight_in: bfloat16 [8, 4, 768, 3072], P('section', 'expert'), may hold values from -0.21875 to 0.21875
- weight_out: bfloat16 [8, 4, 3072, 768], P('section', 'expert'), may hold values from -0.109375 to 0.109375
Outputs:
- layer_states: bfloat16 [8, 16, 32, 768], P('section', None, 'expert')
Inputs may be any that keep to these rules, and one draw needn't show every extreme that they name: `route_ids`: each row names two different experts. In each aligned block of 8 rows (the tokens of one micro-batch on one index of the expert axis) no expert is named by more than 8 rows, and in some blocks one expert is named by exactly 8.
All inputs are finite; a program needn't handle non-finite values.
Results may differ from a plain program's by a relative error of at most 0.028.
Values may be sent and summed in bfloat16 or wider, within the bound.
No kernel may reach another device: no remote copies, remote signals or barrier semaphores. Data moves between devices by JAX's collectives and lax.ppermute only.
A program may use at most 64 MiB of HBM per device.

v0:
```python
import jax
import jax.numpy as jnp
from jax import lax
from jax.sharding import PartitionSpec as P

epsilon = 1e-06


def from_behind(block, axis, distance):
    devices = range(lax.axis_size(axis))
    route = [(i - distance, i) for i in devices if i - distance in devices]
    return lax.ppermute(block, axis, route)


def slot_targets(route_block, experts, capacity):
    owners = route_block.shape[0]
    assigned = route_block.reshape(owners, -1)
    onehot = (assigned[:, :, None] == jnp.arange(experts, dtype=jnp.int32)[None, None, :]).astype(
        jnp.int32
    )
    earlier = jnp.cumsum(onehot, axis=1) - onehot
    position = jnp.sum(onehot * earlier, axis=2)
    return (assigned * capacity + position).reshape(route_block.shape)


def body(tokens, route_ids, router, norm_gain, weight_in, weight_out):
    groups = lax.axis_size("expert")
    sections = lax.axis_size("section")
    section_index = lax.axis_index("section")
    member = lax.axis_index("expert")
    micro_count, tok_rows, features = tokens.shape
    experts = router.shape[2]
    capacity = 4 * tok_rows // experts
    slot_total = experts * capacity
    routes_all = route_ids[0]
    router_block = router[0]
    gain_row = norm_gain[0]
    expert_in = weight_in[0, 0]
    expert_out = weight_out[0, 0]
    columns = jnp.arange(slot_total, dtype=jnp.int32)
    expert_range = jnp.arange(experts, dtype=jnp.int32)
    contract_rows = (((0,), (0,)), ((), ()))

    def apply_expert(received):
        flattened = received.reshape(-1, features)
        hidden = jax.nn.relu(
            jnp.dot(flattened, expert_in, preferred_element_type=jnp.float32)
        ).astype(jnp.bfloat16)
        produced = jnp.dot(hidden, expert_out, preferred_element_type=jnp.float32).astype(
            jnp.bfloat16
        )
        return lax.all_to_all(
            produced.reshape(received.shape), "expert", split_axis=0, concat_axis=0, tiled=True
        )

    def apply_layer(current, route_block):
        stream = current.astype(jnp.float32)
        inverse = lax.rsqrt(jnp.mean(stream * stream, axis=-1, keepdims=True) + epsilon)
        normed = (stream * inverse * gain_row).astype(jnp.bfloat16)
        logits = jnp.dot(normed, router_block, preferred_element_type=jnp.float32)
        owners_block = route_block.reshape(groups, tok_rows, 2)
        targets = slot_targets(owners_block, experts, capacity)
        own_targets = lax.dynamic_index_in_dim(targets, member, 0, keepdims=False)
        own_experts = lax.dynamic_index_in_dim(owners_block, member, 0, keepdims=False)
        selector = (own_targets[:, :, None] == columns[None, None, :]).astype(jnp.bfloat16)
        owner_base = jnp.arange(groups, dtype=jnp.int32)[:, None, None] * capacity
        place = jnp.where(owners_block == member, owner_base + targets - member * capacity, -1)
        receive_columns = jnp.arange(groups * capacity, dtype=jnp.int32)
        picker = jnp.sum(
            (place[..., None] == receive_columns[None, None, None, :]).astype(jnp.bfloat16), axis=2
        )
        picker = picker.reshape(groups * tok_rows, groups * capacity)
        collected = lax.dot_general(
            picker,
            lax.all_gather(normed, "expert", axis=0, tiled=True),
            contract_rows,
            preferred_element_type=jnp.float32,
        )
        returned = apply_expert(collected.astype(jnp.bfloat16).reshape(groups, capacity, features))
        picked = jnp.einsum(
            "tkr,rd->tkd",
            selector,
            returned.reshape(slot_total, features),
            preferred_element_type=jnp.float32,
        )
        chosen = (own_experts[:, :, None] == expert_range[None, None, :]).astype(jnp.float32)
        gate_values = jax.nn.sigmoid(jnp.sum(chosen * logits[:, None, :], axis=2))
        mixed = stream + gate_values[:, 0:1] * picked[:, 0] + gate_values[:, 1:2] * picked[:, 1]
        return mixed.astype(jnp.bfloat16)

    def relay_turn(counter, state_pair):
        received, states = state_pair
        offset_turn = counter - section_index
        active_turn = jnp.logical_and(offset_turn >= 0, offset_turn < micro_count)
        micro_index = jnp.clip(offset_turn, 0, micro_count - 1)
        entering = lax.dynamic_index_in_dim(tokens, micro_index, 0, keepdims=False)
        current = jnp.where(section_index == 0, entering, received)
        route_block = lax.dynamic_index_in_dim(routes_all, micro_index, 0, keepdims=False)
        result = apply_layer(current, route_block)
        previous = lax.dynamic_index_in_dim(states, micro_index, 0, keepdims=False)
        states = lax.dynamic_update_index_in_dim(
            states, jnp.where(active_turn, result, previous), micro_index, 0
        )
        received = from_behind(result, "section", 1)
        return (received, states)

    initial = (
        jnp.zeros((tok_rows, features), jnp.bfloat16),
        jnp.zeros((micro_count, tok_rows, features), jnp.bfloat16),
    )
    leftover, states = lax.fori_loop(0, micro_count + sections - 1, relay_turn, initial)
    return states[None]


def solution(mesh):
    placed = (
        P(None, "expert", None),
        P("section", None, None, None),
        P("section", None, None),
        P("section", None),
        P("section", "expert", None, None),
        P("section", "expert", None, None),
    )
    return jax.shard_map(
        body,
        mesh=mesh,
        in_specs=placed,
        out_specs=P("section", None, "expert", None),
        check_vma=False,
    )
```

profile of v0, /device:TPU:24, one launch (start us, length us, event | category | flops | bytes accessed | tf_op | source)
XLA Modules:
  0.0 645.4 jit_solution(5879649925889089358)
XLA Ops:
  0.9 643.8 %while.18 = (s32[]{:T(128)}, bf16[8,768]{1,0:T(8,128)(2,1)S(1)}, bf16[16,8,768]{2,1,0:T(8,128)(2,1)S(1)}, pred[]{:T(512)}, s32[]{:T(128)}, /*index=5*/bf16[16,8,...) while((s32[]{:T(128)}, bf16[8,768]{1,0:T(8,128)(2,1)S(1)}, ...), condition=%wide.region_6.7_spmd.clone, body=%wide.region_0.6_spmd.clone.sunk | while | flops 304748096 | bytes 10243028 | solution.py:111
  8.9 6.0 fusion.62
  36.9 6.0 fusion.62
  64.9 6.0 fusion.62
  92.9 6.0 fusion.62
  120.8 6.0 fusion.62
  148.8 6.0 fusion.62
  176.8 6.0 fusion.62
  204.8 6.0 fusion.62
  232.8 6.0 fusion.62
  260.8 6.0 fusion.62
  288.8 6.0 fusion.62
  316.8 6.0 fusion.62
  344.8 6.0 fusion.62
  372.8 6.0 fusion.62
  400.7 6.0 fusion.62
  428.7 6.0 fusion.62
  456.7 6.0 fusion.62
  484.7 6.0 fusion.62
  512.7 6.0 fusion.62
  540.7 6.0 fusion.62
  568.7 6.0 fusion.62
  596.7 6.0 fusion.62
  624.7 6.0 fusion.62
  (764 shorter events, 504.3 us)
Async XLA Ops:
  14.9 7.3 %all-to-all-start = ((bf16[4,8,768]{2,1,0:T(8,128)(2,1)}), bf16[4,8,768]{2,1,0:T(8,128)(2,1)S(1)}, u32[]{:S(2)}, u32[]{:S(2)}) async-start(bf16[4,8,768]{2,1,0:T(8,128)(2,1)} %fusion.62), calls=%async_computation | async-start | bytes 98304 | tf_op jit(solution)/shard_map/while/body/eval_jaxpr/all_to_all | solution.py:52
  42.9 7.3 %all-to-all-start = ((bf16[4,8,768]{2,1,0:T(8,128)(2,1)}), bf16[4,8,768]{2,1,0:T(8,128)(2,1)S(1)}, u32[]{:S(2)}, u32[]{:S(2)}) async-start(bf16[4,8,768]{2,1,0:T(8,128)(2,1)} %fusion.62), calls=%async_computation | async-start | bytes 98304 | tf_op jit(solution)/shard_map/while/body/eval_jaxpr/all_to_all | solution.py:52
  70.9 7.3 %all-to-all-start = ((bf16[4,8,768]{2,1,0:T(8,128)(2,1)}), bf16[4,8,768]{2,1,0:T(8,128)(2,1)S(1)}, u32[]{:S(2)}, u32[]{:S(2)}) async-start(bf16[4,8,768]{2,1,0:T(8,128)(2,1)} %fusion.62), calls=%async_computation | async-start | bytes 98304 | tf_op jit(solution)/shard_map/while/body/eval_jaxpr/all_to_all | solution.py:52
  98.9 7.3 %all-to-all-start = ((bf16[4,8,768]{2,1,0:T(8,128)(2,1)}), bf16[4,8,768]{2,1,0:T(8,128)(2,1)S(1)}, u32[]{:S(2)}, u32[]{:S(2)}) async-start(bf16[4,8,768]{2,1,0:T(8,128)(2,1)} %fusion.62), calls=%async_computation | async-start | bytes 98304 | tf_op jit(solution)/shard_map/while/body/eval_jaxpr/all_to_all | solution.py:52
  126.9 7.3 %all-to-all-start = ((bf16[4,8,768]{2,1,0:T(8,128)(2,1)}), bf16[4,8,768]{2,1,0:T(8,128)(2,1)S(1)}, u32[]{:S(2)}, u32[]{:S(2)}) async-start(bf16[4,8,768]{2,1,0:T(8,128)(2,1)} %fusion.62), calls=%async_computation | async-start | bytes 98304 | tf_op jit(solution)/shard_map/while/body/eval_jaxpr/all_to_all | solution.py:52
  154.9 7.3 %all-to-all-start = ((bf16[4,8,768]{2,1,0:T(8,128)(2,1)}), bf16[4,8,768]{2,1,0:T(8,128)(2,1)S(1)}, u32[]{:S(2)}, u32[]{:S(2)}) async-start(bf16[4,8,768]{2,1,0:T(8,128)(2,1)} %fusion.62), calls=%async_computation | async-start | bytes 98304 | tf_op jit(solution)/shard_map/while/body/eval_jaxpr/all_to_all | solution.py:52
  182.9 7.3 %all-to-all-start = ((bf16[4,8,768]{2,1,0:T(8,128)(2,1)}), bf16[4,8,768]{2,1,0:T(8,128)(2,1)S(1)}, u32[]{:S(2)}, u32[]{:S(2)}) async-start(bf16[4,8,768]{2,1,0:T(8,128)(2,1)} %fusion.62), calls=%async_computation | async-start | bytes 98304 | tf_op jit(solution)/shard_map/while/body/eval_jaxpr/all_to_all | solution.py:52
  210.9 7.3 %all-to-all-start = ((bf16[4,8,768]{2,1,0:T(8,128)(2,1)}), bf16[4,8,768]{2,1,0:T(8,128)(2,1)S(1)}, u32[]{:S(2)}, u32[]{:S(2)}) async-start(bf16[4,8,768]{2,1,0:T(8,128)(2,1)} %fusion.62), calls=%async_computation | async-start | bytes 98304 | tf_op jit(solution)/shard_map/while/body/eval_jaxpr/all_to_all | solution.py:52
  238.8 7.3 %all-to-all-start = ((bf16[4,8,768]{2,1,0:T(8,128)(2,1)}), bf16[4,8,768]{2,1,0:T(8,128)(2,1)S(1)}, u32[]{:S(2)}, u32[]{:S(2)}) async-start(bf16[4,8,768]{2,1,0:T(8,128)(2,1)} %fusion.62), calls=%async_computation | async-start | bytes 98304 | tf_op jit(solution)/shard_map/while/body/eval_jaxpr/all_to_all | solution.py:52
  266.8 7.3 %all-to-all-start = ((bf16[4,8,768]{2,1,0:T(8,128)(2,1)}), bf16[4,8,768]{2,1,0:T(8,128)(2,1)S(1)}, u32[]{:S(2)}, u32[]{:S(2)}) async-start(bf16[4,8,768]{2,1,0:T(8,128)(2,1)} %fusion.62), calls=%async_computation | async-start | bytes 98304 | tf_op jit(solution)/shard_map/while/body/eval_jaxpr/all_to_all | solution.py:52
  294.8 7.3 %all-to-all-start = ((bf16[4,8,768]{2,1,0:T(8,128)(2,1)}), bf16[4,8,768]{2,1,0:T(8,128)(2,1)S(1)}, u32[]{:S(2)}, u32[]{:S(2)}) async-start(bf16[4,8,768]{2,1,0:T(8,128)(2,1)} %fusion.62), calls=%async_computation | async-start | bytes 98304 | tf_op jit(solution)/shard_map/while/body/eval_jaxpr/all_to_all | solution.py:52
  322.8 7.3 %all-to-all-start = ((bf16[4,8,768]{2,1,0:T(8,128)(2,1)}), bf16[4,8,768]{2,1,0:T(8,128)(2,1)S(1)}, u32[]{:S(2)}, u32[]{:S(2)}) async-start(bf16[4,8,768]{2,1,0:T(8,128)(2,1)} %fusion.62), calls=%async_computation | async-start | bytes 98304 | tf_op jit(solution)/shard_map/while/body/eval_jaxpr/all_to_all | solution.py:52
  350.8 7.3 %all-to-all-start = ((bf16[4,8,768]{2,1,0:T(8,128)(2,1)}), bf16[4,8,768]{2,1,0:T(8,128)(2,1)S(1)}, u32[]{:S(2)}, u32[]{:S(2)}) async-start(bf16[4,8,768]{2,1,0:T(8,128)(2,1)} %fusion.62), calls=%async_computation | async-start | bytes 98304 | tf_op jit(solution)/shard_map/while/body/eval_jaxpr/all_to_all | solution.py:52
  378.8 7.3 %all-to-all-start = ((bf16[4,8,768]{2,1,0:T(8,128)(2,1)}), bf16[4,8,768]{2,1,0:T(8,128)(2,1)S(1)}, u32[]{:S(2)}, u32[]{:S(2)}) async-start(bf16[4,8,768]{2,1,0:T(8,128)(2,1)} %fusion.62), calls=%async_computation | async-start | bytes 98304 | tf_op jit(solution)/shard_map/while/body/eval_jaxpr/all_to_all | solution.py:52
  406.8 7.3 %all-to-all-start = ((bf16[4,8,768]{2,1,0:T(8,128)(2,1)}), bf16[4,8,768]{2,1,0:T(8,128)(2,1)S(1)}, u32[]{:S(2)}, u32[]{:S(2)}) async-start(bf16[4,8,768]{2,1,0:T(8,128)(2,1)} %fusion.62), calls=%async_computation | async-start | bytes 98304 | tf_op jit(solution)/shard_map/while/body/eval_jaxpr/all_to_all | solution.py:52
  414.3 6.5 %collective-permute-start = (bf16[8,768]{1,0:T(8,128)(2,1)S(1)}, bf16[8,768]{1,0:T(8,128)(2,1)S(1)}, u32[]{:S(2)}, u32[]{:S(2)}) collective-permute-start(bf16[8,768]{1,0:T(8,128)(2,1)S(1)} %get-tuple-element.505), channel_id=1, source_target_pairs={{0,4},{4,8},{8,12},{12,16},{16,20},{20,24},{24,28},{1,5},{5,9},{9,... | collective-permute-start | bytes 36872 | tf_op jit(solution)/shard_map/while/body/eval_jaxpr/ppermute | solution.py:12
  434.8 7.3 %all-to-all-start = ((bf16[4,8,768]{2,1,0:T(8,128)(2,1)}), bf16[4,8,768]{2,1,0:T(8,128)(2,1)S(1)}, u32[]{:S(2)}, u32[]{:S(2)}) async-start(bf16[4,8,768]{2,1,0:T(8,128)(2,1)} %fusion.62), calls=%async_computation | async-start | bytes 98304 | tf_op jit(solution)/shard_map/while/body/eval_jaxpr/all_to_all | solution.py:52
  462.8 7.3 %all-to-all-start = ((bf16[4,8,768]{2,1,0:T(8,128)(2,1)}), bf16[4,8,768]{2,1,0:T(8,128)(2,1)S(1)}, u32[]{:S(2)}, u32[]{:S(2)}) async-start(bf16[4,8,768]{2,1,0:T(8,128)(2,1)} %fusion.62), calls=%async_computation | async-start | bytes 98304 | tf_op jit(solution)/shard_map/while/body/eval_jaxpr/all_to_all | solution.py:52
  490.8 7.3 %all-to-all-start = ((bf16[4,8,768]{2,1,0:T(8,128)(2,1)}), bf16[4,8,768]{2,1,0:T(8,128)(2,1)S(1)}, u32[]{:S(2)}, u32[]{:S(2)}) async-start(bf16[4,8,768]{2,1,0:T(8,128)(2,1)} %fusion.62), calls=%async_computation | async-start | bytes 98304 | tf_op jit(solution)/shard_map/while/body/eval_jaxpr/all_to_all | solution.py:52
  518.7 7.3 %all-to-all-start = ((bf16[4,8,768]{2,1,0:T(8,128)(2,1)}), bf16[4,8,768]{2,1,0:T(8,128)(2,1)S(1)}, u32[]{:S(2)}, u32[]{:S(2)}) async-start(bf16[4,8,768]{2,1,0:T(8,128)(2,1)} %fusion.62), calls=%async_computation | async-start | bytes 98304 | tf_op jit(solution)/shard_map/while/body/eval_jaxpr/all_to_all | solution.py:52
  546.7 7.3 %all-to-all-start = ((bf16[4,8,768]{2,1,0:T(8,128)(2,1)}), bf16[4,8,768]{2,1,0:T(8,128)(2,1)S(1)}, u32[]{:S(2)}, u32[]{:S(2)}) async-start(bf16[4,8,768]{2,1,0:T(8,128)(2,1)} %fusion.62), calls=%async_computation | async-start | bytes 98304 | tf_op jit(solution)/shard_map/while/body/eval_jaxpr/all_to_all | solution.py:52
  574.7 7.3 %all-to-all-start = ((bf16[4,8,768]{2,1,0:T(8,128)(2,1)}), bf16[4,8,768]{2,1,0:T(8,128)(2,1)S(1)}, u32[]{:S(2)}, u32[]{:S(2)}) async-start(bf16[4,8,768]{2,1,0:T(8,128)(2,1)} %fusion.62), calls=%async_computation | async-start | bytes 98304 | tf_op jit(solution)/shard_map/while/body/eval_jaxpr/all_to_all | solution.py:52
  602.7 7.3 %all-to-all-start = ((bf16[4,8,768]{2,1,0:T(8,128)(2,1)}), bf16[4,8,768]{2,1,0:T(8,128)(2,1)S(1)}, u32[]{:S(2)}, u32[]{:S(2)}) async-start(bf16[4,8,768]{2,1,0:T(8,128)(2,1)} %fusion.62), calls=%async_computation | async-start | bytes 98304 | tf_op jit(solution)/shard_map/while/body/eval_jaxpr/all_to_all | solution.py:52
  630.7 7.3 %all-to-all-start = ((bf16[4,8,768]{2,1,0:T(8,128)(2,1)}), bf16[4,8,768]{2,1,0:T(8,128)(2,1)S(1)}, u32[]{:S(2)}, u32[]{:S(2)}) async-start(bf16[4,8,768]{2,1,0:T(8,128)(2,1)} %fusion.62), calls=%async_computation | async-start | bytes 98304 | tf_op jit(solution)/shard_map/while/body/eval_jaxpr/all_to_all | solution.py:52
  (46 other events, 358.0 us)
where the time goes:
time: 651 us; the launch traced here: 645 us
  waiting for transfers between devices  190 us (29%)
  matrix products  150 us (23%)
  starting transfers between devices  121 us (19%)
  blocking collectives  120 us (18%)
  other arithmetic  51.5 us (8%)
  local copies, waits for them, and re-layouts  10.7 us (2%)
    dot_general x23, matrix products, apply_expert(): jnp.dot(hidden, expert_out, preferred_element_type=jnp.float32)  139 us
    all_gather x23, blocking collectives, apply_layer(): lax.all_gather(normed, 'expert', axis=0, tiled=True)  120 us
    ppermute x23, waiting for transfers between devices, from_behind(): return lax.ppermute(block, axis, route)  103 us
    all_to_all x23, waiting for transfers between devices, apply_expert(): lax.all_to_all(produced.reshape(received.shape), 'expert', split_axis=0,...  87.2 us
    all_to_all x23, starting transfers between devices, apply_expert(): lax.all_to_all(produced.reshape(received.shape), 'expert', split_axis=0,...  75.3 us
    ppermute x23, starting transfers between devices, from_behind(): return lax.ppermute(block, axis, route)  46 us
    reduce_sum x23, other arithmetic, apply_layer(): jnp.mean(stream * stream, axis=-1, keepdims=True) + epsilon  19.2 us
    mul x23, other arithmetic, apply_layer(): normed = (stream * inverse * gain_row).astype(jnp.bfloat16)  16.1 us
  transfers between devices with their start and end apart: 46, of which 46 were waited for; matrix products, arithmetic and copies ran while one was open for 1% of the time, Pallas kernels for 0%

commit v1 on v0

--- a/solution.py
+++ b/solution.py
@@ -4,6 +4,19 @@
 from jax.sharding import PartitionSpec as P
 
 epsilon = 1e-06
+
+
+def collect(value, axis, dim):
+    size, mine, rows = (lax.axis_size(axis), lax.axis_index(axis), value.shape[dim])
+    ahead = [(i, (i + 1) % size) for i in range(size)]
+    filled = jnp.zeros((*value.shape[:dim], size * rows, *value.shape[dim + 1 :]), value.dtype)
+    held = value
+    for step in range(size):
+        owner = (mine - step) % size
+        filled = lax.dynamic_update_slice_in_dim(filled, held, owner * rows, axis=dim)
+        if step < size - 1:
+            held = lax.ppermute(held, axis, ahead)
+    return filled
 
 
 def from_behind(block, axis, distance):
@@ -71,10 +84,7 @@
         )
         picker = picker.reshape(groups * tok_rows, groups * capacity)
         collected = lax.dot_general(
-            picker,
-            lax.all_gather(normed, "expert", axis=0, tiled=True),
-            contract_rows,
-            preferred_element_type=jnp.float32,
+            picker, collect(normed, "expert", 0), contract_rows, preferred_element_type=jnp.float32
         )
         returned = apply_expert(collected.astype(jnp.bfloat16).reshape(groups, capacity, features))
         picked = jnp.einsum(

time: 651 us -> 728 us (1.12)
  waiting for transfers between devices: 190 us -> 366 us
  blocking collectives: 120 us -> 0 us
  matrix products: 150 us -> 166 us
    ppermute x0 -> x69, waiting for transfers between devices: none -> 172 us  [collect(): held = lax.ppermute(held, axis, ahead)]
    all_gather x23 -> x0, blocking collectives: 120 us -> none  [apply_layer(): lax.all_gather(normed, 'expert', axis=0, tiled=True)]
    dot_general x23, matrix products: 2.74 us -> 18.8 us  [apply_layer(): logits = jnp.dot(normed, router_block, preferred_element_type=jnp.float32)]
  transfers between devices with their start and end apart: 46 -> 115, of which waited for: 46 -> 115; matrix products, arithmetic and copies ran while one was open for 1% -> 6% of each run, Pallas kernels for 0% -> 0%
where the time goes in v1:
time: 728 us; the launch traced here: 721 us
  waiting for transfers between devices  366 us (50%)
  matrix products  166 us (23%)
  starting transfers between devices  122 us (17%)
  other arithmetic  51.3 us (7%)
  local copies, waits for them, and re-layouts  11.3 us (2%)
    ppermute x69, waiting for transfers between devices, collect(): held = lax.ppermute(held, axis, ahead)  172 us
    dot_general x23, matrix products, apply_expert(): jnp.dot(hidden, expert_out, preferred_element_type=jnp.float32)  139 us
    ppermute x23, waiting for transfers between devices, from_behind(): return lax.ppermute(block, axis, route)  103 us
    all_to_all x23, waiting for transfers between devices, apply_expert(): lax.all_to_all(produced.reshape(received.shape), 'expert', split_axis=0,...  91.3 us
    all_to_all x23, starting transfers between devices, apply_expert(): lax.all_to_all(produced.reshape(received.shape), 'expert', split_axis=0,...  75.3 us
    ppermute x23, starting transfers between devices, from_behind(): return lax.ppermute(block, axis, route)  46 us
    reduce_sum x23, other arithmetic, apply_layer(): jnp.mean(stream * stream, axis=-1, keepdims=True) + epsilon  19 us
    dot_general x23, matrix products, apply_layer(): logits = jnp.dot(normed, router_block, preferred_element_type=jnp.float32)  18.8 us
  transfers between devices with their start and end apart: 115, of which 115 were waited for; matrix products, arithmetic and copies ran while one was open for 6% of the time, Pallas kernels for 0%

profile of v1, /device:TPU:24, one launch (start us, length us, event | category | flops | bytes accessed | tf_op | source)
XLA Modules:
  0.0 720.6 jit_solution(15762747977893608392)
XLA Ops:
  0.9 719.0 %while.18 = (s32[]{:T(128)}, bf16[8,768]{1,0:T(8,128)(2,1)S(1)}, bf16[16,8,768]{2,1,0:T(8,128)(2,1)S(1)}, pred[]{:T(512)}, s32[]{:T(128)}, /*index=5*/bf16[16,8,...) while((s32[]{:T(128)}, bf16[8,768]{1,0:T(8,128)(2,1)S(1)}, ...), condition=%wide.region_6.7_spmd.clone, body=%wide.region_0.6_spmd.clone.sunk | while | flops 304748160 | bytes 10441998 | solution.py:121
  12.1 6.0 fusion.61
  43.4 6.0 fusion.61
  74.7 6.0 fusion.61
  105.9 6.0 fusion.61
  137.2 6.0 fusion.61
  168.4 6.0 fusion.61
  199.7 6.0 fusion.61
  231.0 6.0 fusion.61
  262.2 6.0 fusion.61
  293.5 6.0 fusion.61
  324.7 6.0 fusion.61
  356.0 6.0 fusion.61
  387.2 6.0 fusion.61
  418.5 6.0 fusion.61
  449.8 6.0 fusion.61
  481.0 6.0 fusion.61
  512.3 6.0 fusion.61
  543.5 6.0 fusion.61
  574.8 6.0 fusion.61
  606.0 6.0 fusion.61
  637.3 6.0 fusion.61
  668.6 6.0 fusion.61
  699.8 6.0 fusion.61
  (925 shorter events, 577.4 us)
Async XLA Ops:
  18.2 7.3 %all-to-all-start = ((bf16[4,8,768]{2,1,0:T(8,128)(2,1)}), bf16[4,8,768]{2,1,0:T(8,128)(2,1)S(1)}, u32[]{:S(2)}, u32[]{:S(2)}) async-start(bf16[4,8,768]{2,1,0:T(8,128)(2,1)} %fusion.61), calls=%async_computation | async-start | bytes 98304 | tf_op jit(solution)/shard_map/while/body/eval_jaxpr/all_to_all | solution.py:65
  49.4 7.3 %all-to-all-start = ((bf16[4,8,768]{2,1,0:T(8,128)(2,1)}), bf16[4,8,768]{2,1,0:T(8,128)(2,1)S(1)}, u32[]{:S(2)}, u32[]{:S(2)}) async-start(bf16[4,8,768]{2,1,0:T(8,128)(2,1)} %fusion.61), calls=%async_computation | async-start | bytes 98304 | tf_op jit(solution)/shard_map/while/body/eval_jaxpr/all_to_all | solution.py:65
  80.7 7.3 %all-to-all-start = ((bf16[4,8,768]{2,1,0:T(8,128)(2,1)}), bf16[4,8,768]{2,1,0:T(8,128)(2,1)S(1)}, u32[]{:S(2)}, u32[]{:S(2)}) async-start(bf16[4,8,768]{2,1,0:T(8,128)(2,1)} %fusion.61), calls=%async_computation | async-start | bytes 98304 | tf_op jit(solution)/shard_map/while/body/eval_jaxpr/all_to_all | solution.py:65
  112.0 7.3 %all-to-all-start = ((bf16[4,8,768]{2,1,0:T(8,128)(2,1)}), bf16[4,8,768]{2,1,0:T(8,128)(2,1)S(1)}, u32[]{:S(2)}, u32[]{:S(2)}) async-start(bf16[4,8,768]{2,1,0:T(8,128)(2,1)} %fusion.61), calls=%async_computation | async-start | bytes 98304 | tf_op jit(solution)/shard_map/while/body/eval_jaxpr/all_to_all | solution.py:65
  143.2 7.3 %all-to-all-start = ((bf16[4,8,768]{2,1,0:T(8,128)(2,1)}), bf16[4,8,768]{2,1,0:T(8,128)(2,1)S(1)}, u32[]{:S(2)}, u32[]{:S(2)}) async-start(bf16[4,8,768]{2,1,0:T(8,128)(2,1)} %fusion.61), calls=%async_computation | async-start | bytes 98304 | tf_op jit(solution)/shard_map/while/body/eval_jaxpr/all_to_all | solution.py:65
  174.5 7.3 %all-to-all-start = ((bf16[4,8,768]{2,1,0:T(8,128)(2,1)}), bf16[4,8,768]{2,1,0:T(8,128)(2,1)S(1)}, u32[]{:S(2)}, u32[]{:S(2)}) async-start(bf16[4,8,768]{2,1,0:T(8,128)(2,1)} %fusion.61), calls=%async_computation | async-start | bytes 98304 | tf_op jit(solution)/shard_map/while/body/eval_jaxpr/all_to_all | solution.py:65
  205.7 7.3 %all-to-all-start = ((bf16[4,8,768]{2,1,0:T(8,128)(2,1)}), bf16[4,8,768]{2,1,0:T(8,128)(2,1)S(1)}, u32[]{:S(2)}, u32[]{:S(2)}) async-start(bf16[4,8,768]{2,1,0:T(8,128)(2,1)} %fusion.61), calls=%async_computation | async-start | bytes 98304 | tf_op jit(solution)/shard_map/while/body/eval_jaxpr/all_to_all | solution.py:65
  237.0 7.3 %all-to-all-start = ((bf16[4,8,768]{2,1,0:T(8,128)(2,1)}), bf16[4,8,768]{2,1,0:T(8,128)(2,1)S(1)}, u32[]{:S(2)}, u32[]{:S(2)}) async-start(bf16[4,8,768]{2,1,0:T(8,128)(2,1)} %fusion.61), calls=%async_computation | async-start | bytes 98304 | tf_op jit(solution)/shard_map/while/body/eval_jaxpr/all_to_all | solution.py:65
  268.3 7.3 %all-to-all-start = ((bf16[4,8,768]{2,1,0:T(8,128)(2,1)}), bf16[4,8,768]{2,1,0:T(8,128)(2,1)S(1)}, u32[]{:S(2)}, u32[]{:S(2)}) async-start(bf16[4,8,768]{2,1,0:T(8,128)(2,1)} %fusion.61), calls=%async_computation | async-start | bytes 98304 | tf_op jit(solution)/shard_map/while/body/eval_jaxpr/all_to_all | solution.py:65
  299.5 7.3 %all-to-all-start = ((bf16[4,8,768]{2,1,0:T(8,128)(2,1)}), bf16[4,8,768]{2,1,0:T(8,128)(2,1)S(1)}, u32[]{:S(2)}, u32[]{:S(2)}) async-start(bf16[4,8,768]{2,1,0:T(8,128)(2,1)} %fusion.61), calls=%async_computation | async-start | bytes 98304 | tf_op jit(solution)/shard_map/while/body/eval_jaxpr/all_to_all | solution.py:65
  330.8 7.3 %all-to-all-start = ((bf16[4,8,768]{2,1,0:T(8,128)(2,1)}), bf16[4,8,768]{2,1,0:T(8,128)(2,1)S(1)}, u32[]{:S(2)}, u32[]{:S(2)}) async-start(bf16[4,8,768]{2,1,0:T(8,128)(2,1)} %fusion.61), calls=%async_computation | async-start | bytes 98304 | tf_op jit(solution)/shard_map/while/body/eval_jaxpr/all_to_all | solution.py:65
  362.0 7.3 %all-to-all-start = ((bf16[4,8,768]{2,1,0:T(8,128)(2,1)}), bf16[4,8,768]{2,1,0:T(8,128)(2,1)S(1)}, u32[]{:S(2)}, u32[]{:S(2)}) async-start(bf16[4,8,768]{2,1,0:T(8,128)(2,1)} %fusion.61), calls=%async_computation | async-start | bytes 98304 | tf_op jit(solution)/shard_map/while/body/eval_jaxpr/all_to_all | solution.py:65
  369.6 6.5 collective-permute-start.3
  393.3 7.3 %all-to-all-start = ((bf16[4,8,768]{2,1,0:T(8,128)(2,1)}), bf16[4,8,768]{2,1,0:T(8,128)(2,1)S(1)}, u32[]{:S(2)}, u32[]{:S(2)}) async-start(bf16[4,8,768]{2,1,0:T(8,128)(2,1)} %fusion.61), calls=%async_computation | async-start | bytes 98304 | tf_op jit(solution)/shard_map/while/body/eval_jaxpr/all_to_all | solution.py:65
  424.5 7.3 %all-to-all-start = ((bf16[4,8,768]{2,1,0:T(8,128)(2,1)}), bf16[4,8,768]{2,1,0:T(8,128)(2,1)S(1)}, u32[]{:S(2)}, u32[]{:S(2)}) async-start(bf16[4,8,768]{2,1,0:T(8,128)(2,1)} %fusion.61), calls=%async_computation | async-start | bytes 98304 | tf_op jit(solution)/shard_map/while/body/eval_jaxpr/all_to_all | solution.py:65
  455.8 7.3 %all-to-all-start = ((bf16[4,8,768]{2,1,0:T(8,128)(2,1)}), bf16[4,8,768]{2,1,0:T(8,128)(2,1)S(1)}, u32[]{:S(2)}, u32[]{:S(2)}) async-start(bf16[4,8,768]{2,1,0:T(8,128)(2,1)} %fusion.61), calls=%async_computation | async-start | bytes 98304 | tf_op jit(solution)/shard_map/while/body/eval_jaxpr/all_to_all | solution.py:65
  487.1 7.3 %all-to-all-start = ((bf16[4,8,768]{2,1,0:T(8,128)(2,1)}), bf16[4,8,768]{2,1,0:T(8,128)(2,1)S(1)}, u32[]{:S(2)}, u32[]{:S(2)}) async-start(bf16[4,8,768]{2,1,0:T(8,128)(2,1)} %fusion.61), calls=%async_computation | async-start | bytes 98304 | tf_op jit(solution)/shard_map/while/body/eval_jaxpr/all_to_all | solution.py:65
  518.3 7.3 %all-to-all-start = ((bf16[4,8,768]{2,1,0:T(8,128)(2,1)}), bf16[4,8,768]{2,1,0:T(8,128)(2,1)S(1)}, u32[]{:S(2)}, u32[]{:S(2)}) async-start(bf16[4,8,768]{2,1,0:T(8,128)(2,1)} %fusion.61), calls=%async_computation | async-start | bytes 98304 | tf_op jit(solution)/shard_map/while/body/eval_jaxpr/all_to_all | solution.py:65
  549.6 7.3 %all-to-all-start = ((bf16[4,8,768]{2,1,0:T(8,128)(2,1)}), bf16[4,8,768]{2,1,0:T(8,128)(2,1)S(1)}, u32[]{:S(2)}, u32[]{:S(2)}) async-start(bf16[4,8,768]{2,1,0:T(8,128)(2,1)} %fusion.61), calls=%async_computation | async-start | bytes 98304 | tf_op jit(solution)/shard_map/while/body/eval_jaxpr/all_to_all | solution.py:65
  580.8 7.3 %all-to-all-start = ((bf16[4,8,768]{2,1,0:T(8,128)(2,1)}), bf16[4,8,768]{2,1,0:T(8,128)(2,1)S(1)}, u32[]{:S(2)}, u32[]{:S(2)}) async-start(bf16[4,8,768]{2,1,0:T(8,128)(2,1)} %fusion.61), calls=%async_computation | async-start | bytes 98304 | tf_op jit(solution)/shard_map/while/body/eval_jaxpr/all_to_all | solution.py:65
  612.1 7.3 %all-to-all-start = ((bf16[4,8,768]{2,1,0:T(8,128)(2,1)}), bf16[4,8,768]{2,1,0:T(8,128)(2,1)S(1)}, u32[]{:S(2)}, u32[]{:S(2)}) async-start(bf16[4,8,768]{2,1,0:T(8,128)(2,1)} %fusion.61), calls=%async_computation | async-start | bytes 98304 | tf_op jit(solution)/shard_map/while/body/eval_jaxpr/all_to_all | solution.py:65
  643.3 7.3 %all-to-all-start = ((bf16[4,8,768]{2,1,0:T(8,128)(2,1)}), bf16[4,8,768]{2,1,0:T(8,128)(2,1)S(1)}, u32[]{:S(2)}, u32[]{:S(2)}) async-start(bf16[4,8,768]{2,1,0:T(8,128)(2,1)} %fusion.61), calls=%async_computation | async-start | bytes 98304 | tf_op jit(solution)/shard_map/while/body/eval_jaxpr/all_to_all | solution.py:65
  674.6 7.3 %all-to-all-start = ((bf16[4,8,768]{2,1,0:T(8,128)(2,1)}), bf16[4,8,768]{2,1,0:T(8,128)(2,1)S(1)}, u32[]{:S(2)}, u32[]{:S(2)}) async-start(bf16[4,8,768]{2,1,0:T(8,128)(2,1)} %fusion.61), calls=%async_computation | async-start | bytes 98304 | tf_op jit(solution)/shard_map/while/body/eval_jaxpr/all_to_all | solution.py:65
  705.9 7.3 %all-to-all-start = ((bf16[4,8,768]{2,1,0:T(8,128)(2,1)}), bf16[4,8,768]{2,1,0:T(8,128)(2,1)S(1)}, u32[]{:S(2)}, u32[]{:S(2)}) async-start(bf16[4,8,768]{2,1,0:T(8,128)(2,1)} %fusion.61), calls=%async_computation | async-start | bytes 98304 | tf_op jit(solution)/shard_map/while/body/eval_jaxpr/all_to_all | solution.py:65
  (92 other events, 358.5 us)
